TPU v7x, 512 devices: a 4x2x32 block of a 4x16x32 slice. The times are simulated.
512 devices in a mesh: groups: 2 (over y), expert: 64 (over z, core), hidden: 4 (over x).
Axes of the slice: x: 4, y: 2, z: 32, core: 2. Of those that a mesh axis runs over, the one named last changes fastest.
The devices are a block of a 4x16x32 slice.
Arguments:
- tokens: bfloat16 [2048, 4096], P(('groups', 'expert')), parts along dimension 0, may hold values from -6 to 6
- expert_ids: int32 [2048, 8], P(('groups', 'expert')), parts along dimension 0, may hold values from 0 to 31, all different within a row; in each aligned block of 16 rows (0 to 15, 16 to 31, ...) at most 8 rows name the same one
- router_scores: float32 [2048, 8], P(('groups', 'expert')), parts along dimension 0, may hold values from 0.05 to 1
- gate_weight: bfloat16 [64, 4096, 512], P('expert', None, 'hidden'), may hold values from -0.09375 to 0.09375
- up_weight: bfloat16 [64, 4096, 512], P('expert', None, 'hidden'), may hold values from -0.09375 to 0.09375
- down_weight: bfloat16 [64, 512, 4096], P('expert', 'hidden'), may hold values from -0.1875 to 0.1875
Outputs:
- moe_out: bfloat16 [2048, 4096], P(('groups', 'expert'), 'hidden'), parts along dimension 0
There are 2 independent parts, one for each index of `groups`. A program takes and returns all parts, laid end to end along the dimension named above; an argument that names none is the same for every part. Nothing has to cross between parts.
Inputs may be any that keep to these rules, and one draw needn't show every extreme that they name: `expert_ids`: each row names 8 different experts. In each aligned block of 16 rows no expert is named by more than 8 rows, a bound that some block reaches.
All inputs are finite; a program needn't handle non-finite values.
Results may differ from a plain program's by a relative error of at most 0.012.
Values may be sent and summed in bfloat16 or wider, within the bound.
No kernel may reach another device: no remote copies, remote signals or barrier semaphores. Data moves between devices by JAX's collectives and lax.ppermute only.
A program may use at most 64 MiB of HBM per device.

v0:
```python
import jax
import jax.numpy as jnp
from jax import lax
from jax.sharding import PartitionSpec as P

SPAN = 2


def body(tokens, expert_ids, router_scores, gate_weight, up_weight, down_weight):
    experts = lax.axis_size("expert") // SPAN
    rows = lax.all_gather(tokens, "expert", axis=0, tiled=True)
    routed = 2.5 * router_scores / jnp.sum(router_scores, axis=1, keepdims=True)
    named = expert_ids[:, :, None] == jnp.arange(experts, dtype=jnp.int32)[None, None, :]
    weight_table = jnp.sum(jnp.where(named, routed[:, :, None], 0.0), axis=1)
    weights_all = lax.all_gather(weight_table, "expert", axis=0, tiled=True)
    mine = lax.axis_index("expert") // SPAN
    weight_col = lax.dynamic_slice_in_dim(weights_all, mine, 1, 1)
    down = lax.all_to_all(down_weight[0], "hidden", split_axis=1, concat_axis=0, tiled=True)
    both = jnp.concatenate([gate_weight[0], up_weight[0]], axis=1)
    width = gate_weight.shape[2]
    val = jnp.dot(rows, both, preferred_element_type=jnp.float32)
    act = (jax.nn.silu(val[:, :width]) * val[:, width:]).astype(jnp.bfloat16)
    act_all = lax.all_gather(act, "hidden", axis=1, tiled=True)
    out = jnp.dot(act_all, down, preferred_element_type=jnp.float32)
    out = (out * weight_col).astype(jnp.bfloat16)
    return lax.psum_scatter(out, "expert", scatter_dimension=0, tiled=True)


def solution(mesh):
    return jax.shard_map(
        body,
        mesh=mesh,
        in_specs=(
            P(("groups", "expert"), None),
            P(("groups", "expert"), None),
            P(("groups", "expert"), None),
            P("expert", None, "hidden"),
            P("expert", None, "hidden"),
            P("expert", "hidden", None),
        ),
        out_specs=P(("groups", "expert"), "hidden"),
        check_vma=False,
    )
```

profile of v0, /device:TPU:34, one launch (start us, length us, event | category | flops | bytes accessed | tf_op | source)
XLA Modules:
  0.0 459.3 jit_solution(4400639572138969000)
XLA Ops:
  6.5 0.0 all-gather.3.cloned.1.call-start
  6.6 0.7 all-gather.3.cloned.1.call-update
  7.3 0.1 all-gather.5.cloned.1.call-start
  7.4 167.8 %all-gather.3.cloned.1.call-done = bf16[1024,4096]{1,0:T(8,128)(2,1)} async-done(((bf16[16,4096]{1,0:T(8,128)(2,1)}), bf16[1024,4096]{1,0:T(8,128)(2,1)}) %all-gather.3.cloned.1.call-update) | async-done | bytes 8388624 | tf_op jit(solution)/shard_map/all_gather | solution.py:11
  175.2 0.0 copy-start
  175.2 6.5 %fusion.4 = f32[1024,256]{0,1:T(8,128)S(1)} fusion(bf16[1024,4096]{1,0:T(8,128)(2,1)} %all-gather.3.cloned.1.call-done, bf16[4096,128]{1,0:T(8,128)(2,1)} %bitcast.12, bf16[4096,128]{1,0:T(8,128)(2,1)} %bitcast.13), kind=kOutput, calls=%fused_computation.5 | convolution fusion | flops 2151677952 | bytes 11534336 | tf_op jit(solution)/shard_map/dot_general | solution.py:21
  181.7 0.0 copy-start.1
  181.7 0.0 copy-start.2
  181.7 0.9 fusion.7
  182.6 0.1 all-gather.5.cloned.1.call-update
  182.6 0.0 copy-done
  182.7 1.3 copy.19
  184.0 5.2 %all-to-all-start = ((bf16[128,4,1024]{0,2,1:T(8,128)(2,1)}), bf16[128,4,1024]{0,2,1:T(8,128)(2,1)S(1)}, u32[]{:S(2)}, u32[]{:S(2)}) async-start(bf16[128,4,1024]{0,2,1:T(8,128)(2,1)} %bitcast.3), calls=%async_computation | async-start | bytes 2097152 | tf_op jit(solution)/shard_map/all_to_all | solution.py:18
  189.2 0.0 reduce-scatter.2.cloned.1.call-start
  189.2 0.0 copy-done.1
  189.2 0.1 copy.22
  189.3 0.0 copy-done.2
  189.3 0.1 copy.21
  189.4 0.1 select_reduce_fusion
  189.5 54.6 %all_gather.11 = f32[1024,32]{1,0:T(8,128)S(1)} all-gather(f32[16,32]{1,0:T(8,128)S(1)} %select_reduce_fusion), channel_id=1, replica_groups=mesh['groups'=2,'expert'=64,'hidden'=4] {'expert'}, dimensions={0}, use_global_device_ids=true | all-gather | bytes 133120 | tf_op jit(solution)/shard_map/all_gather | solution.py:15
  244.1 0.4 dynamic-slice_reduce_fusion
  244.5 0.0 all-to-all-done
  244.5 0.5 copy.20
  245.0 0.0 all-gather.5.cloned.1.call-done
  245.0 3.9 multiply_convert_fusion
  248.9 0.1 reduce-scatter.2.cloned.1.call-update
  249.0 203.8 %reduce-scatter.2.cloned.1.call-done = bf16[16,1024]{1,0:T(8,128)(2,1)} async-done(((bf16[1024,1024]{1,0:T(8,128)(2,1)}), bf16[16,1024]{1,0:T(8,128)(2,1)}) %reduce-scatter.2.cloned.1.call-update) | async-done | bytes 32784 | tf_op jit(solution)/shard_map/reduce_scatter | solution.py:26
  (2 shorter events, 0.0 us)
Async XLA Ops:
  6.5 168.7 %all-gather.3.cloned.1.call-start = ((), (), s32[]{:S(2)}) async-start(), calls=%async_computation.2 | async-start | bytes 8519680 | tf_op jit(solution)/shard_map/all_gather | solution.py:11
  7.3 237.7 %all-gather.5.cloned.1.call-start = ((), (), s32[]{:S(2)}) async-start(), calls=%async_computation.3 | async-start | bytes 1310720 | tf_op jit(solution)/shard_map/all_gather | solution.py:23
  175.2 7.4 %copy-start = (bf16[1,128,4096]{2,1,0:T(8,128)(2,1)S(1)}, bf16[1,128,4096]{2,1,0:T(8,128)(2,1)}, u32[]{:S(2)}) copy-start(bf16[1,128,4096]{2,1,0:T(8,128)(2,1)} %param.11) | copy-start | bytes 3145732
  181.7 7.5 %copy-start.1 = (f32[16,8]{0,1:T(8,128)S(1)}, f32[16,8]{0,1:T(8,128)}, u32[]{:S(2)}) copy-start(f32[16,8]{0,1:T(8,128)} %param.8) | copy-start | bytes 1540
  181.7 7.6 %copy-start.2 = (s32[16,8]{0,1:T(8,128)S(1)}, s32[16,8]{0,1:T(8,128)}, u32[]{:S(2)}) copy-start(s32[16,8]{0,1:T(8,128)} %param.7) | copy-start | bytes 1540
  184.0 60.5 %all-to-all-start = ((bf16[128,4,1024]{0,2,1:T(8,128)(2,1)}), bf16[128,4,1024]{0,2,1:T(8,128)(2,1)S(1)}, u32[]{:S(2)}, u32[]{:S(2)}) async-start(bf16[128,4,1024]{0,2,1:T(8,128)(2,1)} %bitcast.3), calls=%async_computation | async-start | bytes 2097152 | tf_op jit(solution)/shard_map/all_to_all | solution.py:18
  189.2 263.6 %reduce-scatter.2.cloned.1.call-start = ((), (), s32[]{:S(2)}) async-start(), calls=%async_computation.4 | async-start | bytes 2129920 | tf_op jit(solution)/shard_map/reduce_scatter | solution.py:26
Sparse Core Ops, SparseCore 0:
  9.5 165.6 all-gather.2
  182.8 30.5 all-gather.4
  249.1 203.5 reduce-scatter.1
where the time goes:
time: 459 us
  waiting for transfers between devices  372 us (81%)
  blocking collectives  54.6 us (12%)
  between operations  13.2 us (3%)
  matrix products  10.3 us (2%)
  starting transfers between devices  5.27 us (1%)
    reduce_scatter x1, waiting for transfers between devices, body(): return lax.psum_scatter(out, 'expert', scatter_dimension=0, tiled=True)  204 us
    all_gather x1, waiting for transfers between devices, body(): rows = lax.all_gather(tokens, 'expert', axis=0, tiled=True)  168 us
    all_gather x1, blocking collectives, body(): weights_all = lax.all_gather(weight_table, 'expert', axis=0, tiled=True)  54.6 us
  transfers between devices with their start and end apart: 4, of which 2 were waited for; matrix products, arithmetic and copies ran while one was open for 1% of the time, Pallas kernels for 0%

commit v1 on v0

--- a/solution.py
+++ b/solution.py
@@ -12,7 +12,9 @@
     routed = 2.5 * router_scores / jnp.sum(router_scores, axis=1, keepdims=True)
     named = expert_ids[:, :, None] == jnp.arange(experts, dtype=jnp.int32)[None, None, :]
     weight_table = jnp.sum(jnp.where(named, routed[:, :, None], 0.0), axis=1)
-    weights_all = lax.all_gather(weight_table, "expert", axis=0, tiled=True)
+    weights_all = jnp.concatenate(
+        lax.all_to_all(jnp.stack([weight_table] * lax.axis_size("expert")), "expert", 0, 0), axis=0
+    )
     mine = lax.axis_index("expert") // SPAN
     weight_col = lax.dynamic_slice_in_dim(weights_all, mine, 1, 1)
     down = lax.all_to_all(down_weight[0], "hidden", split_axis=1, concat_axis=0, tiled=True)

time: 459 us -> 438 us (0.954)
  blocking collectives: 54.6 us -> 0 us
  starting transfers between devices: 5.27 us -> 58.6 us
  waiting for transfers between devices: 372 us -> 349 us
    all_gather x1 -> x0, blocking collectives: 54.6 us -> none  [body(): weights_all = lax.all_gather(weight_table, 'expert', axis=0, tiled=True)]
    all_gather x1, waiting for transfers between devices: 168 us -> 122 us  [body(): rows = lax.all_gather(tokens, 'expert', axis=0, tiled=True)]
    all_to_all x1, starting transfers between devices: 5.2 us -> 43.9 us  [body(): lax.all_to_all(down_weight[0], 'hidden', split_axis=1, concat_axis=0, til...]
    all_to_all x0 -> x1, waiting for transfers between devices: none -> 29.8 us  [body(): lax.all_to_all(jnp.stack([weight_table] * lax.axis_size('expert')), 'expe...]
    all_to_all x0 -> x1, starting transfers between devices: none -> 14.6 us  [body(): lax.all_to_all(jnp.stack([weight_table] * lax.axis_size('expert')), 'expe...]
    reduce_scatter x1, waiting for transfers between devices: 204 us -> 196 us  [body(): return lax.psum_scatter(out, 'expert', scatter_dimension=0, tiled=True)]
  transfers between devices with their start and end apart: 4 -> 5, of which waited for: 2 -> 3; matrix products, arithmetic and copies ran while one was open for 1% -> 3% of each run, Pallas kernels for 0% -> 0%
where the time goes in v1:
time: 438 us; the launch traced here: 437 us
  waiting for transfers between devices  349 us (80%)
  starting transfers between devices  58.6 us (13%)
  between operations  13.2 us (3%)
  matrix products  9.73 us (2%)
  local copies, waits for them, and re-layouts  5.02 us (1%)
    reduce_scatter x1, waiting for transfers between devices, body(): return lax.psum_scatter(out, 'expert', scatter_dimension=0, tiled=True)  196 us
    all_gather x1, waiting for transfers between devices, body(): rows = lax.all_gather(tokens, 'expert', axis=0, tiled=True)  122 us
    all_to_all x1, starting transfers between devices, body(): lax.all_to_all(down_weight[0], 'hidden', split_axis=1, concat_axis=0, til...  43.9 us
    all_to_all x1, waiting for transfers between devices, body(): lax.all_to_all(jnp.stack([weight_table] * lax.axis_size('expert')), 'expe...  29.8 us
    all_to_all x1, starting transfers between devices, body(): lax.all_to_all(jnp.stack([weight_table] * lax.axis_size('expert')), 'expe...  14.6 us
  transfers between devices with their start and end apart: 5, of which 3 were waited for; matrix products, arithmetic and copies ran while one was open for 3% of the time, Pallas kernels for 0%

profile of v1, /device:TPU:34, one launch (start us, length us, event | category | flops | bytes accessed | tf_op | source)
XLA Modules:
  0.0 437.3 jit_solution(12405510523816569268)
XLA Ops:
  6.5 0.0 copy-start.2
  6.5 0.0 copy-start.3
  6.6 0.0 all-gather.3.cloned.1.call-start
  6.6 0.7 all-gather.3.cloned.1.call-update
  7.3 2.3 copy.15
  9.6 43.9 %all-to-all-start = ((bf16[128,4,1024]{0,2,1:T(8,128)(2,1)}), bf16[128,4,1024]{0,2,1:T(8,128)(2,1)S(1)}, u32[]{:S(2)}, u32[]{:S(2)}) async-start(bf16[128,4,1024]{0,2,1:T(8,128)(2,1)} %bitcast.3), calls=%async_computation | async-start | bytes 2097152 | tf_op jit(solution)/shard_map/all_to_all | solution.py:20
  53.5 0.0 all-gather.5.cloned.1.call-start
  53.5 121.7 %all-gather.3.cloned.1.call-done = bf16[1024,4096]{1,0:T(8,128)(2,1)} async-done(((bf16[16,4096]{1,0:T(8,128)(2,1)}), bf16[1024,4096]{1,0:T(8,128)(2,1)}) %all-gather.3.cloned.1.call-update) | async-done | bytes 8388624 | tf_op jit(solution)/shard_map/all_gather | solution.py:11
  175.2 0.0 copy-done.2
  175.2 0.0 copy-done.3
  175.2 0.0 copy-start
  175.2 0.0 copy-start.1
  175.2 5.9 %fusion.4 = f32[1024,256]{0,1:T(8,128)S(1)} fusion(bf16[1024,4096]{1,0:T(8,128)(2,1)} %all-gather.3.cloned.1.call-done, bf16[4096,128]{1,0:T(8,128)(2,1)S(1)} %bitcast.14, bf16[4096,128]{1,0:T(8,128)(2,1)S(1)} %bitcast.15), kind=kOutput, calls=%fused_computation.5 | convolution fusion | flops 2151677952 | bytes 11534336 | tf_op jit(solution)/shard_map/dot_general | solution.py:23
  181.1 0.8 fusion.7
  182.0 0.1 all-gather.5.cloned.1.call-update
  182.0 0.0 copy-done
  182.1 0.1 copy.18
  182.1 0.0 copy-done.1
  182.1 0.1 copy.17
  182.2 0.1 select_reduce_fusion
  182.4 0.9 reshape.14
  183.3 0.0 all-to-all-done
  183.3 14.6 %all-to-all-start.1 = ((f32[64,1,512]{2,1,0:T(1,128)}), f32[64,1,512]{2,1,0:T(1,128)S(1)}, u32[]{:S(2)}, u32[]{:S(2)}) async-start(f32[64,1,512]{2,1,0:T(1,128)} %reshape.14), calls=%async_computation.1 | async-start | bytes 262144 | tf_op jit(solution)/shard_map/all_to_all | solution.py:16
  198.0 0.1 reduce-scatter.2.cloned.1.call-start
  198.0 0.5 copy.16
  198.6 29.8 %all-to-all-done.1 = f32[64,1,512]{2,1,0:T(1,128)S(1)} async-done(((f32[64,1,512]{2,1,0:T(1,128)}), f32[64,1,512]{2,1,0:T(1,128)S(1)}, u32[]{:S(2)}, u32[]{:S(2)}) %all-to-all-start.1) | async-done | bytes 131104 | tf_op jit(solution)/shard_map/all_to_all | solution.py:16
  228.4 0.5 broadcast.9
  228.9 0.9 reduce.2
  229.9 0.2 reshape.15
  230.0 0.4 dynamic-slice_reduce_fusion
  230.4 0.0 all-gather.5.cloned.1.call-done
  230.4 3.9 multiply_convert_fusion
  234.3 0.1 reduce-scatter.2.cloned.1.call-update
  234.4 196.4 %reduce-scatter.2.cloned.1.call-done = bf16[16,1024]{1,0:T(8,128)(2,1)} async-done(((bf16[1024,1024]{1,0:T(8,128)(2,1)}), bf16[16,1024]{1,0:T(8,128)(2,1)}) %reduce-scatter.2.cloned.1.call-update) | async-done | bytes 32784 | tf_op jit(solution)/shard_map/reduce_scatter | solution.py:28
  (3 shorter events, 0.1 us)
Async XLA Ops:
  6.5 168.7 %copy-start.2 = (bf16[1,4096,128]{2,1,0:T(8,128)(2,1)S(1)}, bf16[1,4096,128]{2,1,0:T(8,128)(2,1)}, u32[]{:S(2)}) copy-start(bf16[1,4096,128]{2,1,0:T(8,128)(2,1)} %param.10) | copy-start | bytes 3145732
  6.5 168.7 %copy-start.3 = (bf16[1,4096,128]{2,1,0:T(8,128)(2,1)S(1)}, bf16[1,4096,128]{2,1,0:T(8,128)(2,1)}, u32[]{:S(2)}) copy-start(bf16[1,4096,128]{2,1,0:T(8,128)(2,1)} %param.9) | copy-start | bytes 3145732
  6.6 168.7 %all-gather.3.cloned.1.call-start = ((), (), s32[]{:S(2)}) async-start(), calls=%async_computation.3 | async-start | bytes 8519680 | tf_op jit(solution)/shard_map/all_gather | solution.py:11
  9.6 173.7 %all-to-all-start = ((bf16[128,4,1024]{0,2,1:T(8,128)(2,1)}), bf16[128,4,1024]{0,2,1:T(8,128)(2,1)S(1)}, u32[]{:S(2)}, u32[]{:S(2)}) async-start(bf16[128,4,1024]{0,2,1:T(8,128)(2,1)} %bitcast.3), calls=%async_computation | async-start | bytes 2097152 | tf_op jit(solution)/shard_map/all_to_all | solution.py:20
  53.5 176.9 %all-gather.5.cloned.1.call-start = ((), (), s32[]{:S(2)}) async-start(), calls=%async_computation.4 | async-start | bytes 1310720 | tf_op jit(solution)/shard_map/all_gather | solution.py:25
  175.2 6.8 %copy-start = (f32[16,8]{0,1:T(8,128)S(1)}, f32[16,8]{0,1:T(8,128)}, u32[]{:S(2)}) copy-start(f32[16,8]{0,1:T(8,128)} %param.8) | copy-start | bytes 1540
  175.2 6.9 %copy-start.1 = (s32[16,8]{0,1:T(8,128)S(1)}, s32[16,8]{0,1:T(8,128)}, u32[]{:S(2)}) copy-start(s32[16,8]{0,1:T(8,128)} %param.7) | copy-start | bytes 1540
  183.3 45.1 %all-to-all-start.1 = ((f32[64,1,512]{2,1,0:T(1,128)}), f32[64,1,512]{2,1,0:T(1,128)S(1)}, u32[]{:S(2)}, u32[]{:S(2)}) async-start(f32[64,1,512]{2,1,0:T(1,128)} %reshape.14), calls=%async_computation.1 | async-start | bytes 262144 | tf_op jit(solution)/shard_map/all_to_all | solution.py:16
  198.0 232.8 %reduce-scatter.2.cloned.1.call-start = ((), (), s32[]{:S(2)}) async-start(), calls=%async_computation.5 | async-start | bytes 2129920 | tf_op jit(solution)/shard_map/reduce_scatter | solution.py:28
Sparse Core Ops, SparseCore 0:
  9.5 165.6 all-gather.2
  182.1 30.8 all-gather.4
  234.5 196.2 reduce-scatter.1
